TPU v7x, 32 devices: a 4x4x1 block of a 4x4x8 slice. The times are simulated.
32 devices in a mesh: dp: 1 (over z), tp: 32 (over y, x, core).
Axes of the slice: x: 4, y: 4, z: 1, core: 2. Of those that a mesh axis runs over, the one named last changes fastest.
The devices are a block of a 4x4x8 slice.
Arguments:
- x: bfloat16 [2048, 4096], P('dp')
- mu1: float32 [2048], P('dp')
- rs1: float32 [2048], P('dp')
- g1: bfloat16 [4096], replicated
- g2: bfloat16 [4096], replicated
- dy: bfloat16 [2048, 4096], P('dp')
- wqkv: bfloat16 [4096, 12288], P(None, 'tp')
- wo: bfloat16 [32, 128, 4096], P('tp')
- w1: bfloat16 [4096, 16384], P(None, 'tp')
- w2: bfloat16 [16384, 4096], P('tp')
Outputs:
- output 1: bfloat16 [2048, 4096], P('dp')
- output 2: bfloat16 [4096, 12288], P('dp', 'tp')
- output 3: bfloat16 [32, 128, 4096], P(('dp', 'tp'))
- output 4: bfloat16 [4096, 16384], P('dp', 'tp')
- output 5: bfloat16 [16384, 4096], P(('dp', 'tp'))
All inputs are finite; a program needn't handle non-finite values.
Results may differ from a plain program's by a relative error of at most 0.0182407.
Values are sent between devices in bfloat16 or wider.
A program may use at most 768 MiB of HBM per device.

v0:
```python
import jax
import jax.numpy as jnp
from jax import lax
from jax.sharding import PartitionSpec as P

EPS = 1.0 / 100000


def _ln_bwd(dn, xh, rs, g):
    u = dn * g
    return rs[..., None] * (u - jnp.mean(u, axis=-1, keepdims=True) - xh * jnp.mean(u * xh, axis=-1, keepdims=True))


def _probs(q, k):
    n = q.shape[0]
    s = jnp.dot(q, k.T, preferred_element_type=jnp.float32) * q.shape[1] ** -0.5
    mask = jnp.arange(n)[:, None] >= jnp.arange(n)[None, :]
    return jax.nn.softmax(jnp.where(mask, s, -jnp.inf), axis=-1)


def _head_fwd(qkv):
    q, k, v = qkv[:, 0], qkv[:, 1], qkv[:, 2]
    p = _probs(q, k)
    return jnp.dot(p.astype(jnp.bfloat16), v, preferred_element_type=jnp.float32).astype(jnp.bfloat16)


def _head_bwd(args):
    qkv, do = args
    q, k, v = qkv[:, 0], qkv[:, 1], qkv[:, 2]
    p = _probs(q, k)
    dv = jnp.dot(p.astype(jnp.bfloat16).T, do, preferred_element_type=jnp.float32)
    dpm = jnp.dot(do, v.T, preferred_element_type=jnp.float32)
    ds = (p * (dpm - jnp.sum(p * dpm, axis=-1, keepdims=True)) * q.shape[1] ** -0.5).astype(jnp.bfloat16)
    dq = jnp.dot(ds, k, preferred_element_type=jnp.float32)
    dk = jnp.dot(ds.T, q, preferred_element_type=jnp.float32)
    return jnp.stack([dq, dk, dv], axis=1).astype(jnp.bfloat16)


def solution(mesh):
    def body(x, mu1, rs1, g1, g2, dy, wqkv, wo, w1, w2):
        f32 = jnp.float32
        bf = jnp.bfloat16
        hl, hd, d = wo.shape
        t = x.shape[0]
        xf = x.astype(f32)
        g1f = g1.astype(f32)
        g2f = g2.astype(f32)
        xh1 = (xf - mu1[:, None]) * rs1[:, None]
        n1 = (xh1 * g1f).astype(bf)
        qkv = jnp.dot(n1, wqkv, preferred_element_type=f32).astype(bf)
        qkv = jnp.moveaxis(qkv.reshape(t, hl, 3, hd), 1, 0)
        o = lax.map(_head_fwd, qkv)
        o = jnp.moveaxis(o, 0, 1).reshape(t, hl * hd)
        wo2 = wo.reshape(hl * hd, d)
        attn = jnp.dot(o, wo2, preferred_element_type=f32).astype(bf)
        h1 = xf + lax.psum(attn, "tp").astype(f32)
        mu2 = jnp.mean(h1, axis=-1, keepdims=True)
        xc = h1 - mu2
        rs2 = lax.rsqrt(jnp.mean(xc * xc, axis=-1) + EPS)
        xh2 = xc * rs2[:, None]
        n2 = (xh2 * g2f).astype(bf)
        a = jnp.dot(n2, w1, preferred_element_type=f32)
        gl, gelu_vjp = jax.vjp(jax.nn.gelu, a)
        gb = gl.astype(bf)
        dw2 = jnp.dot(gb.T, dy, preferred_element_type=f32).astype(bf)
        dg = jnp.dot(dy, w2.T, preferred_element_type=f32)
        da = gelu_vjp(dg)[0].astype(bf)
        dw1 = jnp.dot(n2.T, da, preferred_element_type=f32).astype(bf)
        dn2 = jnp.dot(da, w1.T, preferred_element_type=f32).astype(bf)
        dn2 = lax.psum(dn2, "tp").astype(f32)
        dh1 = dy.astype(f32) + _ln_bwd(dn2, xh2, rs2, g2f)
        dh1b = dh1.astype(bf)
        dwo = jnp.dot(o.T, dh1b, preferred_element_type=f32).astype(bf).reshape(hl, hd, d)
        do = jnp.dot(dh1b, wo2.T, preferred_element_type=f32).astype(bf)
        do = jnp.moveaxis(do.reshape(t, hl, hd), 1, 0)
        dqkv = lax.map(_head_bwd, (qkv, do))
        dqkv = jnp.moveaxis(dqkv, 0, 1).reshape(t, 3 * hl * hd)
        dwqkv = jnp.dot(n1.T, dqkv, preferred_element_type=f32).astype(bf)
        dn1 = jnp.dot(dqkv, wqkv.T, preferred_element_type=f32).astype(bf)
        dn1 = lax.psum(dn1, "tp").astype(f32)
        dx = (dh1 + _ln_bwd(dn1, xh1, rs1, g1f)).astype(bf)
        return dx, dwqkv, dwo, dw1, dw2

    return jax.shard_map(
        body, mesh=mesh,
        in_specs=(P("dp", None), P("dp"), P("dp"), P(None), P(None), P("dp", None),
                  P(None, "tp"), P("tp", None, None), P(None, "tp"), P("tp", None)),
        out_specs=(P("dp", None), P("dp", "tp"), P(("dp", "tp"), None, None), P("dp", "tp"), P(("dp", "tp"), None)),
        check_vma=False)
```

profile of v0, /device:TPU:97, one launch (start us, length us, event | category | flops | bytes accessed | tf_op | source)
XLA Modules:
  0.0 813.3 jit_solution(1013785552765659175)
XLA Ops:
  8.7 16.9 %fusion.4 = bf16[2048,4096]{1,0:T(8,128)(2,1)} fusion(bf16[2048,4096]{1,0:T(8,128)(2,1)} %param.10, f32[4096]{0:T(1024)S(1)} %convert_element_type.88, f32[2048]{0:T(1024)} %param.12, f32[2048]{0:T(1024)} %param.11), kind=kLoop, calls=%fused_computation.6 | loop fusion | flops 41943040 | bytes 33587200 | tf_op jit(solution)/shard_map/convert_element_type | solution.py:49
  25.7 10.6 %convolution_convert_fusion.6 = bf16[2048,384]{0,1:T(8,128)(2,1)S(1)} fusion(bf16[2048,4096]{1,0:T(8,128)(2,1)} %fusion.4, bf16[4096,384]{1,0:T(8,128)(2,1)S(1)} %copy-done), kind=kOutput, calls=%fused_computation.57 | convolution fusion | flops 6443237376 | bytes 21495808 | tf_op jit(solution)/shard_map/dot_general | solution.py:50
  60.6 15.0 %fusion.67 = f32[2048,512]{1,0:T(8,128)} fusion(bf16[2048,4096]{1,0:T(8,128)(2,1)} %param.15, bf16[512,4096]{1,0:T(8,128)(2,1)} %param.19), kind=kOutput, calls=%fused_computation.88 | convolution fusion | flops 8589934592 | bytes 25165824 | tf_op jit(solution)/shard_map/dot_general | solution.py:66
  75.6 155.4 %all-reduce.4.cloned.1.call-done = bf16[2048,4096]{1,0:T(8,128)(2,1)} async-done(((bf16[2048,4096]{1,0:T(8,128)(2,1)}), bf16[2048,4096]{1,0:T(8,128)(2,1)}) %all-reduce.4.cloned.1.call-update) | async-done | bytes 16777232 | tf_op jit(solution)/shard_map/psum | solution.py:56
  231.0 15.5 %fusion.13 = f32[2048]{0:T(1024)S(1)} fusion(bf16[2048,4096]{1,0:T(8,128)(2,1)} %all-reduce.4.cloned.1.call-done, bf16[2048,4096]{1,0:T(8,128)(2,1)} %param.10), kind=kLoop, calls=%fused_computation.21 | loop fusion | flops 33552384 | bytes 33562624 | tf_op jit(solution)/shard_map/reduce_sum | solution.py:57
  246.6 14.0 %multiply_reduce_fusion.1 = f32[2048]{0:T(1024)S(1)} fusion(bf16[2048,4096]{1,0:T(8,128)(2,1)S(1)} %copy-done.1, bf16[2048,4096]{1,0:T(8,128)(2,1)} %param.10, f32[2048]{0:T(1024)S(1)} %broadcast_multiply_fusion.4), kind=kLoop, calls=%fused_computation.19 | loop fusion | flops 50329600 | bytes 33570816 | tf_op jit(solution)/shard_map/reduce_sum | solution.py:59
  260.6 11.9 %multiply_convert_fusion = bf16[2048,4096]{1,0:T(8,128)(2,1)} fusion(bf16[2048,4096]{1,0:T(8,128)(2,1)S(1)} %copy-done.1, bf16[2048,4096]{1,0:T(8,128)(2,1)S(1)} %bitcast.55, f32[4096]{0:T(1024)S(1)} %convert_element_type.95, f32[2048]{0:T(1024)S(1)} %add_rsqrt_fusion, f32[2048]{0:T(1024)S(1)} %broadcast_multiply_fusion.4), kind=kLoop, calls=%fused_computation.18 | loop fusion | flops 58720256 | bytes 50364416 | tf_op jit(solution)/shard_map/convert_element_type | solution.py:61
  272.5 18.2 %fusion.34 = (bf16[2048,512]{1,0:T(8,128)(2,1)}, f32[2048,512]{1,0:T(8,128)}) fusion(f32[2048,512]{1,0:T(8,128)} %fusion.67, bf16[2048,4096]{1,0:T(8,128)(2,1)} %multiply_convert_fusion, bf16[4096,512]{1,0:T(8,128)(2,1)} %param.18), kind=kOutput, calls=%fused_computation.51 | convolution fusion | flops 8610906112 | bytes 31457280 | tf_op jit(solution)/shard_map/dot_general | solution.py:62
  290.7 14.4 %convolution_convert_fusion = bf16[2048,4096]{1,0:T(8,128)(2,1)} fusion(bf16[2048,512]{1,0:T(8,128)(2,1)} %get-tuple-element.32, bf16[4096,512]{1,0:T(8,128)(2,1)S(1)} %copy-done.18), kind=kOutput, calls=%fused_computation.28 | convolution fusion | flops 8598323200 | bytes 23068672 | tf_op jit(solution)/shard_map/dot_general | solution.py:69
  305.2 167.1 %all-reduce.6.cloned.1.call-done = bf16[2048,4096]{1,0:T(8,128)(2,1)} async-done(((bf16[2048,4096]{1,0:T(8,128)(2,1)}), bf16[2048,4096]{1,0:T(8,128)(2,1)}) %all-reduce.6.cloned.1.call-update) | async-done | bytes 16777232 | tf_op jit(solution)/shard_map/psum | solution.py:70
  472.3 20.1 %fusion.11 = (f32[2048]{0:T(1024)S(1)}, f32[2048]{0:T(1024)S(1)}) fusion(bf16[2048,4096]{1,0:T(8,128)(2,1)} %all-reduce.6.cloned.1.call-done, f32[4096]{0:T(1024)S(1)} %convert_element_type.95, f32[2048]{0:T(1024)S(1)} %add_rsqrt_fusion, f32[2048]{0:T(1024)S(1)} %broadcast_multiply_fusion.4, bf16[2048,4096]{1,0:T(8,128)(2,1)} %all-reduce.4.cloned.1.call-done, ...), kind=kLoop, calls=%fused_computation.17 | loop fusion | flops 83881984 | bytes 50380800 | tf_op jit(solution)/shard_map/reduce_sum | solution.py:11
  492.5 33.8 %multiply_add_fusion = f32[2048,4096]{1,0:T(8,128)} fusion(bf16[2048,4096]{1,0:T(8,128)(2,1)} %all-reduce.6.cloned.1.call-done, bf16[2048,4096]{1,0:T(8,128)(2,1)} %param.15, bf16[2048,4096]{1,0:T(8,128)(2,1)} %all-reduce.4.cloned.1.call-done, bf16[2048,4096]{1,0:T(8,128)(2,1)} %param.10, f32[2048]{0:T(1024)S(1)} %get-tuple-element.36, ...), kind=kLoop, calls=%fused_computation.14 | loop fusion | flops 109051904 | bytes 100712448 | tf_op jit(solution)/shard_map/add | solution.py:71
  526.3 16.2 %fusion.45 = bf16[2048,128]{1,0:T(8,128)(2,1)} fusion(f32[2048,4096]{1,0:T(8,128)} %multiply_add_fusion, bf16[1,128,4096]{2,1,0:T(8,128)(2,1)} %param.17), kind=kOutput, calls=%fused_computation.62 | convolution fusion | flops 2156134400 | bytes 35127296 | tf_op jit(solution)/shard_map/dot_general | solution.py:74
  542.5 11.1 %fusion.48 = bf16[2048,1,128]{0,2,1:T(8,128)(2,1)S(1)} fusion(bf16[2048,128]{1,0:T(8,128)(2,1)} %fusion.45, f32[2048,2048]{0,1:T(8,128)} %copy-done.2, f32[2048]{0:T(1024)S(1)} %copy-done.16, f32[2048]{0:T(1024)S(1)} %copy-done.14), kind=kOutput, calls=%fused_computation.63 | convolution fusion | flops 1099169792 | bytes 17842176 | tf_op jit(solution)/shard_map/while/body/eval_jaxpr/dot_general | solution.py:31
  553.7 12.9 %multiply_reduce_fusion.2 = (f32[2048]{0:T(1024)S(1)}, f32[2048,2048]{0,1:T(8,128)}) fusion(f32[2048]{0:T(1024)S(1)} %copy-done.16, f32[2048]{0:T(1024)S(1)} %copy-done.14, f32[2048,2048]{0,1:T(8,128)} %copy-done.2, bf16[2048,128]{1,0:T(8,128)(2,1)S(1)} %copy-done.6, bf16[2048,3,128]{0,2,1:T(8,128)(2,1)} %bitcast.62), kind=kOutput, calls=%fused_computation.24 | convolution fusion | flops 1103099904 | bytes 34627584 | tf_op jit(solution)/shard_map/while/body/eval_jaxpr/dot_general | solution.py:32
  566.6 9.7 %multiply_convert_fusion.1 = bf16[2048,2048]{0,1:T(8,128)(2,1)S(1)} fusion(f32[2048,2048]{0,1:T(8,128)} %get-tuple-element.35, f32[2048]{0:T(1024)S(1)} %get-tuple-element.34, f32[2048]{0:T(1024)S(1)} %copy-done.16, f32[2048]{0:T(1024)S(1)} %copy-done.14, f32[2048,2048]{0,1:T(8,128)S(1)} %bitcast.57), kind=kLoop, calls=%fused_computation.23 | loop fusion | flops 37748736 | bytes 41967616 | tf_op jit(solution)/shard_map/while/body/eval_jaxpr/convert_element_type | solution.py:33
  581.8 12.6 %convolution_convert_fusion.2 = bf16[2048,4096]{1,0:T(8,128)(2,1)} fusion(bf16[2048,384]{0,1:T(8,128)(2,1)S(1)} %bitcast.58, bf16[4096,384]{1,0:T(8,128)(2,1)S(1)} %copy-done), kind=kOutput, calls=%fused_computation.30 | convolution fusion | flops 6450839552 | bytes 21495808 | tf_op jit(solution)/shard_map/dot_general | solution.py:79
  594.5 16.1 %convolution_convert_fusion.3 = bf16[512,4096]{1,0:T(8,128)(2,1)} fusion(bf16[2048,4096]{1,0:T(8,128)(2,1)} %param.15, f32[2048,512]{1,0:T(8,128)} %get-tuple-element.33), kind=kOutput, calls=%fused_computation.40 | convolution fusion | flops 8601468928 | bytes 25165824 | tf_op jit(solution)/shard_map/dot_general | solution.py:65
  610.6 14.2 %convolution_convert_fusion.4 = bf16[4096,512]{1,0:T(8,128)(2,1)} fusion(bf16[2048,4096]{1,0:T(8,128)(2,1)} %multiply_convert_fusion, bf16[2048,512]{1,0:T(8,128)(2,1)S(1)} %copy-done.19), kind=kOutput, calls=%fused_computation.41 | convolution fusion | flops 8592031744 | bytes 23068672 | tf_op jit(solution)/shard_map/dot_general | solution.py:68
  624.8 14.1 %fusion.25 = bf16[1,128,4096]{2,1,0:T(8,128)(2,1)} fusion(bf16[2048,128]{1,0:T(8,128)(2,1)} %copy-done.4, f32[2048,4096]{1,0:T(8,128)} %multiply_add_fusion), kind=kOutput, calls=%fused_computation.44 | convolution fusion | flops 2156396544 | bytes 35127296 | tf_op jit(solution)/shard_map/dot_general | solution.py:73
  638.9 14.2 %convolution_convert_fusion.5 = bf16[4096,384]{1,0:T(8,128)(2,1)} fusion(bf16[2048,4096]{1,0:T(8,128)(2,1)} %fusion.4, bf16[2048,384]{0,1:T(8,128)(2,1)} %bitcast.59), kind=kOutput, calls=%fused_computation.42 | convolution fusion | flops 6444023808 | bytes 21495808 | tf_op jit(solution)/shard_map/dot_general | solution.py:78
  653.1 108.8 %all-reduce.8.cloned.1.call-done = bf16[2048,4096]{1,0:T(8,128)(2,1)} async-done(((bf16[2048,4096]{1,0:T(8,128)(2,1)}), bf16[2048,4096]{1,0:T(8,128)(2,1)}) %all-reduce.8.cloned.1.call-update) | async-done | bytes 16777232 | tf_op jit(solution)/shard_map/psum | solution.py:80
  761.8 16.1 %fusion.10 = (f32[2048]{0:T(1024)S(1)}, f32[2048]{0:T(1024)S(1)}) fusion(bf16[2048,4096]{1,0:T(8,128)(2,1)} %all-reduce.8.cloned.1.call-done, f32[4096]{0:T(1024)S(1)} %copy-done.10, f32[2048]{0:T(1024)S(1)} %copy-done.11, f32[2048]{0:T(1024)S(1)} %copy-done.12, bf16[2048,4096]{1,0:T(8,128)(2,1)} %param.10), kind=kLoop, calls=%fused_computation.13 | loop fusion | flops 67104768 | bytes 33603584 | tf_op jit(solution)/shard_map/reduce_sum | solution.py:11
  778.0 28.3 %fusion.9 = bf16[2048,4096]{1,0:T(8,128)(2,1)} fusion(f32[2048,4096]{1,0:T(8,128)} %multiply_add_fusion, bf16[2048,4096]{1,0:T(8,128)(2,1)} %param.10, bf16[2048,4096]{1,0:T(8,128)(2,1)} %all-reduce.8.cloned.1.call-done, f32[2048]{0:T(1024)S(1)} %broadcast_multiply_fusion, f32[2048]{0:T(1024)S(1)} %broadcast_multiply_fusion.1, f32[4096]{0:T(1024)S(1)} %copy-done.10, ...), kind=kLoop, calls=%fused_computation.11 | loop fusion | flops 92274688 | bytes 83935232 | tf_op jit(solution)/shard_map/convert_element_type | solution.py:81
  (78 shorter events, 31.6 us)
Async XLA Ops:
  7.2 18.5 %copy-start = (bf16[4096,384]{1,0:T(8,128)(2,1)S(1)}, bf16[4096,384]{1,0:T(8,128)(2,1)}, u32[]{:S(2)}) copy-start(bf16[4096,384]{1,0:T(8,128)(2,1)} %param.16) | copy-start | bytes 9437188
  7.2 223.8 %all-reduce.4.cloned.1.call-start = ((), (), s32[]{:S(2)}) async-start(), calls=%async_computation | async-start | bytes 33554432 | tf_op jit(solution)/shard_map/psum | solution.py:56
  45.0 7.3 copy-start.3
  52.2 8.4 %copy-start.17 = (bf16[4096]{0:T(1024)(128)(2,1)S(1)}, bf16[4096]{0:T(1024)(128)(2,1)}, u32[]{:S(2)}) copy-start(bf16[4096]{0:T(1024)(128)(2,1)} %param.14) | copy-start | bytes 24580
  60.5 411.8 %all-reduce.6.cloned.1.call-start = ((), (), s32[]{:S(2)}) async-start(), calls=%async_computation.1 | async-start | bytes 33554432 | tf_op jit(solution)/shard_map/psum | solution.py:70
  231.0 15.5 %copy-start.1 = (bf16[2048,4096]{1,0:T(8,128)(2,1)S(1)}, bf16[2048,4096]{1,0:T(8,128)(2,1)}, u32[]{:S(2)}) copy-start(bf16[2048,4096]{1,0:T(8,128)(2,1)} %all-reduce.4.cloned.1.call-done) | copy-start | bytes 50331652
  231.0 29.6 %slice-start = ((s8[16777216]{0:T(1024)(128)(4,1)}), s8[4194304]{0:T(1024)(128)(4,1)S(1)}, s32[]{:S(2)}) async-start(s8[16777216]{0:T(1024)(128)(4,1)} %bitcast.54), calls=%async_computation.3 | async-start | bytes 8388608
  231.0 29.6 %slice-start.1 = ((s8[16777216]{0:T(1024)(128)(4,1)}), s8[4194304]{0:T(1024)(128)(4,1)S(1)}, s32[]{:S(2)}) async-start(s8[16777216]{0:T(1024)(128)(4,1)} %bitcast.54), calls=%async_computation.4 | async-start | bytes 8388608
  246.5 14.0 %slice-start.2 = ((s8[16777216]{0:T(1024)(128)(4,1)}), s8[4194304]{0:T(1024)(128)(4,1)S(1)}, s32[]{:S(2)}) async-start(s8[16777216]{0:T(1024)(128)(4,1)} %bitcast.54), calls=%async_computation.5 | async-start | bytes 8388608
  246.5 14.0 %slice-start.3 = ((s8[16777216]{0:T(1024)(128)(4,1)}), s8[4194304]{0:T(1024)(128)(4,1)S(1)}, s32[]{:S(2)}) async-start(s8[16777216]{0:T(1024)(128)(4,1)} %bitcast.54), calls=%async_computation.6 | async-start | bytes 8388608
  272.5 18.2 %copy-start.18 = (bf16[4096,512]{1,0:T(8,128)(2,1)S(1)}, bf16[4096,512]{1,0:T(8,128)(2,1)}, u32[]{:S(2)}) copy-start(bf16[4096,512]{1,0:T(8,128)(2,1)} %param.18) | copy-start | bytes 12582916
  305.1 456.7 %all-reduce.8.cloned.1.call-start = ((), (), s32[]{:S(2)}) async-start(), calls=%async_computation.2 | async-start | bytes 33554432 | tf_op jit(solution)/shard_map/psum | solution.py:80
  526.3 16.2 %copy-start.14 = (f32[2048]{0:T(1024)S(1)}, f32[2048]{0:T(1024)}, u32[]{:S(2)}) copy-start(f32[2048]{0:T(1024)} %copy-done.13) | copy-start | bytes 24580
  526.3 16.2 %copy-start.16 = (f32[2048]{0:T(1024)S(1)}, f32[2048]{0:T(1024)}, u32[]{:S(2)}) copy-start(f32[2048]{0:T(1024)} %copy-done.15) | copy-start | bytes 24580
  542.5 11.2 %copy-start.6 = (bf16[2048,128]{1,0:T(8,128)(2,1)S(1)}, bf16[2048,128]{1,0:T(8,128)(2,1)}, u32[]{:S(2)}) copy-start(bf16[2048,128]{1,0:T(8,128)(2,1)} %fusion.45) | copy-start | bytes 1572868
  542.5 24.1 %slice-start.4 = ((s8[16777216]{0:T(1024)(128)(4,1)}), s8[4194304]{0:T(1024)(128)(4,1)S(1)}, s32[]{:S(2)}) async-start(s8[16777216]{0:T(1024)(128)(4,1)} %bitcast.56), calls=%async_computation.7 | async-start | bytes 8388608
  542.5 24.0 %slice-start.5 = ((s8[16777216]{0:T(1024)(128)(4,1)}), s8[4194304]{0:T(1024)(128)(4,1)S(1)}, s32[]{:S(2)}) async-start(s8[16777216]{0:T(1024)(128)(4,1)} %bitcast.56), calls=%async_computation.8 | async-start | bytes 8388608
  553.6 12.9 %slice-start.6 = ((s8[16777216]{0:T(1024)(128)(4,1)}), s8[4194304]{0:T(1024)(128)(4,1)S(1)}, s32[]{:S(2)}) async-start(s8[16777216]{0:T(1024)(128)(4,1)} %bitcast.56), calls=%async_computation.9 | async-start | bytes 8388608
  553.7 12.9 %slice-start.7 = ((s8[16777216]{0:T(1024)(128)(4,1)}), s8[4194304]{0:T(1024)(128)(4,1)S(1)}, s32[]{:S(2)}) async-start(s8[16777216]{0:T(1024)(128)(4,1)} %bitcast.56), calls=%async_computation.10 | async-start | bytes 8388608
  566.6 9.7 %copy-start.8 = (bf16[2048,384]{0,1:T(8,128)(2,1)S(1)}, bf16[2048,384]{0,1:T(8,128)(2,1)}, u32[]{:S(2)}) copy-start(bf16[2048,384]{0,1:T(8,128)(2,1)} %copy-done.7) | copy-start | bytes 4718596
  594.5 16.1 %copy-start.19 = (bf16[2048,512]{1,0:T(8,128)(2,1)S(1)}, bf16[2048,512]{1,0:T(8,128)(2,1)}, u32[]{:S(2)}) copy-start(bf16[2048,512]{1,0:T(8,128)(2,1)} %get-tuple-element.32) | copy-start | bytes 6291460
  638.9 123.0 %copy-start.10 = (f32[4096]{0:T(1024)S(1)}, f32[4096]{0:T(1024)}, u32[]{:S(2)}) copy-start(f32[4096]{0:T(1024)} %copy-done.9) | copy-start | bytes 49156
  638.9 123.0 %copy-start.11 = (f32[2048]{0:T(1024)S(1)}, f32[2048]{0:T(1024)}, u32[]{:S(2)}) copy-start(f32[2048]{0:T(1024)} %param.12) | copy-start | bytes 24580
  638.9 123.0 %copy-start.12 = (f32[2048]{0:T(1024)S(1)}, f32[2048]{0:T(1024)}, u32[]{:S(2)}) copy-start(f32[2048]{0:T(1024)} %param.11) | copy-start | bytes 24580
  (7 other events, 21.7 us)
Sparse Core Ops, SparseCore 0:
  60.6 170.3 all-reduce.3
  305.2 167.0 all-reduce.5
  594.6 167.1 all-reduce.7
where the time goes:
time: 827 us; the launch traced here: 813 us
  waiting for transfers between devices  431 us (52%)
  matrix products  191 us (23%)
  other arithmetic  172 us (21%)
  between operations  14.6 us (2%)
    psum x1, waiting for transfers between devices, body(): dn2 = lax.psum(dn2, 'tp').astype(f32)  167 us
    psum x1, waiting for transfers between devices, body(): h1 = xf + lax.psum(attn, 'tp').astype(f32)  155 us
    psum x1, waiting for transfers between devices, body(): dn1 = lax.psum(dn1, 'tp').astype(f32)  109 us
    reduce_sum x2, other arithmetic, _ln_bwd(): jnp.mean(u, axis=-1, keepdims=True)  36.2 us
    add x1, other arithmetic, body(): dh1 = dy.astype(f32) + _ln_bwd(dn2, xh2, rs2, g2f)  33.8 us
    convert_element_type x1, other arithmetic, body(): dx = (dh1 + _ln_bwd(dn1, xh1, rs1, g1f)).astype(bf)  28.3 us
    dot_general x1, matrix products, body(): a = jnp.dot(n2, w1, preferred_element_type=f32)  18.2 us
    convert_element_type x1, other arithmetic, body(): n1 = (xh1 * g1f).astype(bf)  16.9 us
  transfers between devices with their start and end apart: 3, of which 3 were waited for; matrix products, arithmetic and copies ran while one was open for 9% of the time, Pallas kernels for 0%

commit v1 on v0

v1 whole, which is shorter than its diff:
```python
import functools

import jax
import jax.numpy as jnp
from jax import lax
from jax.experimental import pallas as pl
from jax.experimental.pallas import tpu as pltpu
from jax.sharding import PartitionSpec as P

EPS = 1.0 / 100000
F32 = jnp.float32
BF = jnp.bfloat16
MESH = pl.DeviceIdType.MESH
OFFS = (2, 1, 3, 0)
GOFFS = (0, 3, 1, 2)


def _probs(q, k):
    n = q.shape[0]
    s = jnp.dot(q, k.T, preferred_element_type=F32) * q.shape[1] ** -0.5
    mask = jnp.arange(n)[:, None] >= jnp.arange(n)[None, :]
    return jax.nn.softmax(jnp.where(mask, s, -jnp.inf), axis=-1)


def _head_fwd(qkv):
    q, k, v = qkv[:, 0], qkv[:, 1], qkv[:, 2]
    p = _probs(q, k)
    return jnp.dot(p.astype(BF), v, preferred_element_type=F32).astype(BF)


def _head_bwd(qkv, do):
    q, k, v = qkv[:, 0], qkv[:, 1], qkv[:, 2]
    p = _probs(q, k)
    dv = jnp.dot(p.astype(BF).T, do, preferred_element_type=F32)
    dpm = jnp.dot(do, v.T, preferred_element_type=F32)
    ds = (p * (dpm - jnp.sum(p * dpm, axis=-1, keepdims=True)) * q.shape[1] ** -0.5).astype(BF)
    dq = jnp.dot(ds, k, preferred_element_type=F32)
    dk = jnp.dot(ds.T, q, preferred_element_type=F32)
    return jnp.stack([dq, dk, dv], axis=1).astype(BF)


class _Copy:
    def __init__(self, make):
        self.make = make

    def start(self):
        self.make().start()

    def wait_send(self):
        self.make().wait_send()

    def wait_recv(self):
        self.make().wait_recv()


def _rows(n, step, f):
    @pl.loop(0, n // step)
    def _(i):
        f(pl.ds(pl.multiple_of(i * step, step), step))


def _mid_fwd(total, put, ins, outs):
    x, g2 = ins
    xh_out, rs_out = outs
    n = total.shape[0]

    def f(r):
        h = x[r, :].astype(F32) + total[r, :]
        xc = h - jnp.mean(h, axis=-1, keepdims=True)
        rs = lax.rsqrt(jnp.mean(xc * xc, axis=-1, keepdims=True) + EPS)
        xh = xc * rs
        xh_out[r, :] = xh
        rs_out[r, :] = jnp.broadcast_to(rs, (rs.shape[0], rs_out.shape[1]))
        put(r, (xh * g2[...].astype(F32)).astype(BF))
    _rows(n, 16, f)


def _lnb(dn, xh, rs, g):
    u = dn * g
    return rs * (u - jnp.mean(u, axis=-1, keepdims=True) - xh * jnp.mean(u * xh, axis=-1, keepdims=True))


def _mid_mlp(total, put, ins, outs):
    dy, g2, xh, rs = ins
    (dh_out,) = outs
    n = total.shape[0]

    def f(r):
        dh = dy[r, :].astype(F32) + _lnb(total[r, :], xh[r, :], rs[r, 0:1], g2[...].astype(F32))
        dh_out[r, :] = dh
        put(r, dh.astype(BF))
    _rows(n, 16, f)


def _mid_in(total, put, ins, outs):
    x, g1, mu, rs, dh = ins
    n = total.shape[0]

    def f(r):
        xh = (x[r, :].astype(F32) - mu[r, 0:1]) * rs[r, 0:1]
        dx = dh[r, :] + _lnb(total[r, :], xh, rs[r, 0:1], g1[...].astype(F32))
        put(r, dx.astype(BF))
    _rows(n, 16, f)


def _exchange_kernel(side, trans, mid, n_in, n_out, *refs):
    l_ref, w_ref, wp_ref = refs[:3]
    ins = refs[3:3 + n_in]
    g_ref = refs[3 + n_in]
    outs = refs[4 + n_in:4 + n_in + n_out]
    (lp, pb, ra, rb, q, r2a, r2b, ag, tot,
     sl, s1, r1, s2, r2, gs, gr, hs, hr, ds, dr, os_) = refs[4 + n_in + n_out:]
    n = side
    t, d = ag.shape
    half, unit, b = t // 2, t // (2 * n), t // (2 * n * n)
    hb = b // 2
    me = lax.axis_index("tp")
    c, chip = me % 2, me // 2
    y, x = chip // n, chip % n
    f = (1 - c) * y + c * x
    s = (1 - c) * x + c * y

    def dev(f_, s_):
        return (((1 - c) * f_ + c * s_) * n + (1 - c) * s_ + c * f_) * 2 + c

    fr, fl = dev((f + 1) % n, s), dev((f + n - 1) % n, s)
    sr, sl_ = dev(f, (s + 1) % n), dev(f, (s + n - 1) % n)
    partner = me + 1 - 2 * c

    barrier = pltpu.get_barrier_semaphore()
    for p in (fr, fl, sr, sl_, partner):
        pl.semaphore_signal(barrier, inc=1, device_id={"tp": p}, device_id_type=MESH)
    pl.semaphore_wait(barrier, 5)

    def copy(src, dst, ssem, rsem, to):
        return _Copy(lambda: pltpu.make_async_remote_copy(
            src_ref=src, dst_ref=dst, send_sem=ssem, recv_sem=rsem, device_id={"tp": to}, device_id_type=MESH))

    def blk(k):
        return (f + k) % n

    lx = copy(l_ref.at[pl.ds(pl.multiple_of((1 - c) * half, half), half)], lp, sl.at[0], sl.at[1], partner)
    lx.start()
    lx.wait_recv()

    dims = (((1,), (1,)), ((), ())) if trans else (((1,), (0,)), ((), ()))
    nt = 512

    def product(k):
        sp = (s + OFFS[k]) % n
        own = l_ref[pl.ds(pl.multiple_of(c * half + sp * unit, unit), unit), :]
        oth = lp[pl.ds(pl.multiple_of(sp * unit, unit), unit), :]

        @pl.loop(0, d // nt)
        def _(j):
            cs = pl.ds(pl.multiple_of(j * nt, nt), nt)
            wa = w_ref[cs, :] if trans else w_ref[:, cs]
            wb = wp_ref[cs, :] if trans else wp_ref[:, cs]
            acc = lax.dot_general(own, wa, dims, preferred_element_type=F32)
            acc = acc + lax.dot_general(oth, wb, dims, preferred_element_type=F32)
            acc = acc.astype(BF)
            for i in range(n):
                pb[k, i, :, cs] = acc[i * b:(i + 1) * b]

    def add_rows(dst, src, rows, off):
        @pl.loop(0, rows // 16)
        def _(i):
            rd = pl.ds(pl.multiple_of(off + i * 16, 16), 16)
            rs_ = pl.ds(pl.multiple_of(i * 16, 16), 16)
            dst[rd, :] = (dst[rd, :].astype(F32) + src[rs_, :].astype(F32)).astype(BF)

    def c1a(k):
        o = pb.at[k, blk(2)]
        return (copy(o.at[pl.ds(0, hb)], ra.at[k, 0], s1.at[k, 0], r1.at[k, 0], fr),
                copy(o.at[pl.ds(hb, hb)], ra.at[k, 1], s1.at[k, 1], r1.at[k, 1], fl))

    def c1b(k):
        return (copy(pb.at[k, blk(1)], rb.at[k, 0], s1.at[k, 2], r1.at[k, 2], fr),
                copy(pb.at[k, blk(3)], rb.at[k, 1], s1.at[k, 3], r1.at[k, 3], fl))

    def c2a():
        return (copy(q.at[0, pl.ds(0, hb)], r2a.at[0], s2.at[0], r2.at[0], sr),
                copy(q.at[0, pl.ds(hb, hb)], r2a.at[1], s2.at[1], r2.at[1], sl_))

    def c2b():
        return (copy(q.at[1], r2b.at[0], s2.at[2], r2.at[2], sr),
                copy(q.at[2], r2b.at[1], s2.at[3], r2.at[3], sl_))

    def step_a(k):
        product(k)
        for cp in c1a(k):
            cp.start()

    def step_b(k):
        ca, cb = c1a(k), c1b(k)
        ca[0].wait_recv()
        add_rows(pb.at[k, blk(1)], ra.at[k, 0], hb, 0)
        cb[0].start()
        ca[1].wait_recv()
        add_rows(pb.at[k, blk(3)], ra.at[k, 1], hb, hb)
        cb[1].start()

    def step_c(k):
        for cp in c1b(k):
            cp.wait_recv()
        mine, l, r = pb.at[k, f], rb.at[k, 0], rb.at[k, 1]

        @pl.loop(0, b // 16)
        def _(i):
            rs_ = pl.ds(pl.multiple_of(i * 16, 16), 16)
            v = mine[rs_, :].astype(F32) + l[rs_, :].astype(F32) + r[rs_, :].astype(F32)
            q[k, rs_, :] = v.astype(BF)

    step_a(0)
    step_a(1)
    step_b(0)
    step_a(2)
    step_b(1)
    step_a(3)
    step_b(2)
    step_b(3)
    a2, b2 = c2a(), c2b()
    step_c(0)
    a2[0].start()
    a2[1].start()
    step_c(1)
    a2[0].wait_recv()
    add_rows(q.at[1], r2a.at[0], hb, 0)
    b2[0].start()
    step_c(2)
    a2[1].wait_recv()
    add_rows(q.at[2], r2a.at[1], hb, hb)
    b2[1].start()
    for cp in c1b(3):
        cp.wait_recv()
    b2[0].wait_recv()
    b2[1].wait_recv()

    def final(r):
        tot[r, :] = (pb[3, f, r, :].astype(F32) + rb[3, 0, r, :].astype(F32) + rb[3, 1, r, :].astype(F32)
                     + r2b[0, r, :].astype(F32) + r2b[1, r, :].astype(F32))
    _rows(b, 16, final)

    def row(s_, f_):
        return pl.multiple_of(c * half + s_ * unit + f_ * b, b)

    r0 = row(s, f)

    def put(r, v):
        ag[pl.ds(pl.multiple_of(r0 + r.start, 16), r.size), :] = v
    mid(tot, put, ins, outs)

    def block(row_, off, size):
        return ag.at[pl.ds(pl.multiple_of(row_ + off, hb), size)]

    def gcopy(row_, off, size, ssem, rsem, to):
        return copy(block(row_, off, size), block(row_, off, size), ssem, rsem, to)

    gS = (gcopy(r0, 0, b, gs.at[0], gr.at[0], sr), gcopy(r0, 0, b, gs.at[1], gr.at[1], sl_),
          gcopy(row((s + n - 1) % n, f), 0, hb, gs.at[2], gr.at[2], sr),
          gcopy(row((s + 1) % n, f), hb, hb, gs.at[3], gr.at[3], sl_))

    def urow(u, k):
        return row((s + GOFFS[u]) % n, blk(k))

    def gF(u):
        return (gcopy(urow(u, 0), 0, b, hs.at[u, 0], hr.at[u, 0], fr),
                gcopy(urow(u, 0), 0, b, hs.at[u, 1], hr.at[u, 1], fl),
                gcopy(urow(u, 3), 0, hb, hs.at[u, 2], hr.at[u, 2], fr),
                gcopy(urow(u, 1), hb, hb, hs.at[u, 3], hr.at[u, 3], fl))

    def pair(u, k):
        return gcopy(urow(u, k), 0, b, ds.at[u, k], dr.at[u, k], partner)

    def f1(u):
        g = gF(u)
        g[0].start()
        g[1].start()
        pair(u, 0).start()

    def f2(u):
        g = gF(u)
        g[0].wait_recv()
        g[2].start()
        pair(u, 3).start()
        g[1].wait_recv()
        g[3].start()
        pair(u, 1).start()

    def f3(u):
        g = gF(u)
        g[2].wait_recv()
        g[3].wait_recv()
        pair(u, 2).start()
        out(c * half + ((s + GOFFS[u]) % n) * unit, u).start()

    def out(r_, i):
        sl2 = pl.ds(pl.multiple_of(r_, unit), unit)
        return pltpu.make_async_copy(ag.at[sl2], g_ref.at[sl2], os_.at[i])

    gS[0].start()
    gS[1].start()
    f1(0)
    gS[0].wait_recv()
    gS[2].start()
    f1(1)
    gS[1].wait_recv()
    gS[3].start()
    f1(2)
    f2(0)
    gS[2].wait_recv()
    gS[3].wait_recv()
    f1(3)
    f2(1)
    f3(0)
    f2(2)
    f3(1)
    f2(3)
    f3(2)
    f3(3)

    def theirs(u):
        return (1 - c) * half + ((f + GOFFS[u]) % n) * unit
    for u in range(n):
        for k in range(n):
            pair(u, k).wait_recv()
        out(theirs(u), n + u).start()
    for u in range(n):
        out(c * half + ((s + GOFFS[u]) % n) * unit, u).wait()
        out(theirs(u), n + u).wait()
    lx.wait_send()
    for k in range(n):
        for cp in c1a(k) + c1b(k):
            cp.wait_send()
    for cp in a2 + b2 + gS:
        cp.wait_send()
    for u in range(n):
        for cp in gF(u):
            cp.wait_send()
        for k in range(n):
            pair(u, k).wait_send()


def _exchange(tp, cid, trans, mid, lhs, w, wp, ins, extra):
    side = round((tp // 2) ** 0.5)
    assert side == 4 and side * side * 2 == tp
    n = side
    t, kk = lhs.shape
    d = w.shape[0] if trans else w.shape[1]
    half, b = t // 2, t // tp
    vm = pl.BlockSpec(memory_space=pltpu.VMEM)
    dma = pltpu.SemaphoreType.DMA
    outs = [jax.ShapeDtypeStruct((t, d), BF)] + [jax.ShapeDtypeStruct(s, F32) for s in extra]
    return pl.pallas_call(
        functools.partial(_exchange_kernel, side, trans, mid, len(ins), len(extra)),
        out_shape=outs,
        in_specs=[vm] * (3 + len(ins)),
        out_specs=[pl.BlockSpec(memory_space=pl.ANY)] + [vm] * len(extra),
        scratch_shapes=[
            pltpu.VMEM((half, kk), BF),
            pltpu.VMEM((n, n, b, d), BF),
            pltpu.VMEM((n, 2, b // 2, d), BF),
            pltpu.VMEM((n, 2, b, d), BF),
            pltpu.VMEM((n - 1, b, d), BF),
            pltpu.VMEM((2, b // 2, d), BF),
            pltpu.VMEM((2, b, d), BF),
            pltpu.VMEM((t, d), BF),
            pltpu.VMEM((b, d), F32),
            dma((2,)),
            dma((n, 4)), dma((n, 4)),
            dma((4,)), dma((4,)),
            dma((4,)), dma((4,)),
            dma((n, 4)), dma((n, 4)),
            dma((n, n)), dma((n, n)),
            dma((2 * n,)),
        ],
        compiler_params=pltpu.CompilerParams(collective_id=cid, has_side_effects=True,
                                             vmem_limit_bytes=62 * 1024 * 1024),
        cost_estimate=pl.CostEstimate(flops=2 * t * kk * d * 12, bytes_accessed=t * d * 4, transcendentals=0),
        name=f"exchange{cid}",
    )(lhs, w, wp, *ins)


def solution(mesh):
    tp = mesh.shape["tp"]
    swap = [(i, i + 1 - 2 * (i % 2)) for i in range(tp)]

    def body(x, mu1, rs1, g1, g2, dy, wqkv, wo, w1, w2):
        hl, hd, d = wo.shape
        t = x.shape[0]
        side = round((tp // 2) ** 0.5)
        b = t // tp
        me = lax.axis_index("tp")
        c, chip = me % 2, me // 2
        yy, xx = chip // side, chip % side
        own = c * (t // 2) + ((1 - c) * (xx * side + yy) + c * (yy * side + xx)) * b
        wo2 = wo.reshape(hl * hd, d)
        wo_p = lax.ppermute(wo2, "tp", swap)
        w1_p = lax.ppermute(w1, "tp", swap)
        wqkv_p = lax.ppermute(wqkv, "tp", swap)

        def mine(a):
            return lax.dynamic_slice_in_dim(a, own, b, 0)

        xr, dyr = mine(x), mine(dy)
        mur = jnp.broadcast_to(mine(mu1)[:, None], (b, 128))
        rsr = jnp.broadcast_to(mine(rs1)[:, None], (b, 128))
        g1r, g2r = g1[None, :], g2[None, :]

        xh1 = (x.astype(F32) - mu1[:, None]) * rs1[:, None]
        n1 = (xh1 * g1.astype(F32)).astype(BF)
        qkv = jnp.dot(n1, wqkv, preferred_element_type=F32).astype(BF)
        qkv = jnp.moveaxis(qkv.reshape(t, hl, 3, hd), 1, 0)
        o = jnp.moveaxis(lax.map(_head_fwd, qkv), 0, 1).reshape(t, hl * hd)
        n2, xh2, rs2 = _exchange(tp, 0, False, _mid_fwd, o, wo2, wo_p, [xr, g2r], [(b, d), (b, 128)])
        a = jnp.dot(n2, w1, preferred_element_type=F32)
        gl, gelu_vjp = jax.vjp(jax.nn.gelu, a)
        gb = gl.astype(BF)
        dw2 = jnp.dot(gb.T, dy, preferred_element_type=F32).astype(BF)
        dg = jnp.dot(dy, w2.T, preferred_element_type=F32)
        da = gelu_vjp(dg)[0].astype(BF)
        dw1 = jnp.dot(n2.T, da, preferred_element_type=F32).astype(BF)
        dh1b, dh1 = _exchange(tp, 1, True, _mid_mlp, da, w1, w1_p, [dyr, g2r, xh2, rs2], [(b, d)])
        dwo = jnp.dot(o.T, dh1b, preferred_element_type=F32).astype(BF).reshape(hl, hd, d)
        do = jnp.dot(dh1b, wo2.T, preferred_element_type=F32).astype(BF)
        do = jnp.moveaxis(do.reshape(t, hl, hd), 1, 0)
        dqkv = lax.map(lambda z: _head_bwd(*z), (qkv, do))
        dqkv = jnp.moveaxis(dqkv, 0, 1).reshape(t, 3 * hl * hd)
        dwqkv = jnp.dot(n1.T, dqkv, preferred_element_type=F32).astype(BF)
        (dx,) = _exchange(tp, 2, True, _mid_in, dqkv, wqkv, wqkv_p, [xr, g1r, mur, rsr, dh1], [])
        return dx, dwqkv, dwo, dw1, dw2

    return jax.shard_map(
        body, mesh=mesh,
        in_specs=(P("dp", None), P("dp"), P("dp"), P(None), P(None), P("dp", None),
                  P(None, "tp"), P("tp", None, None), P(None, "tp"), P("tp", None)),
        out_specs=(P("dp", None), P("dp", "tp"), P(("dp", "tp"), None, None), P("dp", "tp"), P(("dp", "tp"), None)),
        check_vma=False)
```

time: 827 us -> 538 us (0.65)
  waiting for transfers between devices: 431 us -> 0.01 us
  Pallas kernels: 0 us -> 332 us
  other arithmetic: 172 us -> 32.3 us
  matrix products: 191 us -> 134 us
  local copies, waits for them, and re-layouts: 4.28 us -> 27.2 us
  between operations: 14.6 us -> 1.12 us
    psum x3 -> x0, waiting for transfers between devices: 431 us -> none  [the longest x1 167 us: body(): dn2 = lax.psum(dn2, 'tp').astype(f32)]
    pallas_call x0 -> x3, Pallas kernels: none -> 332 us  [_exchange(): pl.pallas_call(functools.partial(_exchange_kernel, side, trans, mid, len(...]
    reduce_sum x4 -> x0, other arithmetic: 65.7 us -> none  [the longest x2 36.2 us: _ln_bwd(): jnp.mean(u, axis=-1, keepdims=True)]
    dot_general x17 -> x14, matrix products: 191 us -> 134 us  [the longest x1 17.6 us: body(): a = jnp.dot(n2, w1, preferred_element_type=F32)]
    convert_element_type x5 -> x2, other arithmetic: 58 us -> 17.8 us  [body(): n1 = (xh1 * g1.astype(F32)).astype(BF)]
    add x1 -> x0, other arithmetic: 33.8 us -> none  [body(): dh1 = dy.astype(f32) + _ln_bwd(dn2, xh2, rs2, g2f)]
    unnamed x56 -> x49, local copies, waits for them, and re-layouts: 4.28 us -> 16.7 us
  transfers between devices with their start and end apart: 3 -> 3, of which waited for: 3 -> 0; matrix products, arithmetic and copies ran while one was open for 9% -> 33% of each run, Pallas kernels for 0% -> 42%
where the time goes in v1:
time: 538 us; the launch traced here: 529 us
  Pallas kernels  332 us (62%)
  matrix products  134 us (25%)
  other arithmetic  32.3 us (6%)
  local copies, waits for them, and re-layouts  27.2 us (5%)
    pallas_call x3, Pallas kernels, _exchange(): pl.pallas_call(functools.partial(_exchange_kernel, side, trans, mid, len(...  332 us
    convert_element_type x2, other arithmetic, body(): n1 = (xh1 * g1.astype(F32)).astype(BF)  17.8 us
    dot_general x1, matrix products, body(): a = jnp.dot(n2, w1, preferred_element_type=F32)  17.6 us
    unnamed x49, local copies, waits for them, and re-layouts  16.7 us
    dot_general x1, matrix products, body(): dw2 = jnp.dot(gb.T, dy, preferred_element_type=F32).astype(BF)  15.2 us
    dot_general x1, matrix products, body(): dg = jnp.dot(dy, w2.T, preferred_element_type=F32)  14.1 us
    dot_general x1, matrix products, body(): dwqkv = jnp.dot(n1.T, dqkv, preferred_element_type=F32).astype(BF)  13.7 us
    dot_general x1, matrix products, body(): dw1 = jnp.dot(n2.T, da, preferred_element_type=F32).astype(BF)  13.5 us
  transfers between devices with their start and end apart: 3, of which 0 were waited for; matrix products, arithmetic and copies ran while one was open for 33% of the time, Pallas kernels for 42%

profile of v1, /device:TPU:97, one launch (start us, length us, event | category | flops | bytes accessed | tf_op | source)
XLA Modules:
  0.0 529.3 jit_solution(15294976289275181993)
XLA Ops:
  0.6 2.1 collective-permute-start
  4.0 17.1 %multiply_convert_fusion = bf16[2048,4096]{1,0:T(8,128)(2,1)} fusion(bf16[2048,4096]{1,0:T(8,128)(2,1)} %param.10, f32[4096]{0:T(1024)S(1)} %convert_element_type.54, f32[2048]{0:T(1024)} %param.12, f32[2048]{0:T(1024)} %param.11), kind=kLoop, calls=%fused_computation | loop fusion | flops 41943040 | bytes 33587200 | tf_op jit(solution)/shard_map/convert_element_type | solution.py:411
  21.1 10.7 %convolution_convert_fusion.4 = bf16[2048,384]{0,1:T(8,128)(2,1)S(1)} fusion(bf16[2048,4096]{1,0:T(8,128)(2,1)} %multiply_convert_fusion, bf16[4096,384]{1,0:T(8,128)(2,1)S(1)} %copy-done.13), kind=kOutput, calls=%fused_computation.28 | convolution fusion | flops 6443237376 | bytes 21495808 | tf_op jit(solution)/shard_map/dot_general | solution.py:412
  31.8 2.4 fusion.2
  34.2 4.7 fusion.1
  39.9 7.1 %fusion.15.refs_0_ = bf16[2048,128]{1,0:T(8,128)(2,1)} fusion(bf16[2048,3,128]{0,2,1:T(8,128)(2,1)S(1)} %bitcast.54, f32[2048,2048]{0,1:T(8,128)S(1)} %get-tuple-element.37, f32[2048]{0:T(1024)S(1)} %fusion.1, f32[2048]{0:T(1024)S(1)} %get-tuple-element.36), kind=kOutput, calls=%fused_computation.31 | convolution fusion | flops 1099169792 | bytes 17842176 | tf_op jit(solution)/shard_map/while/body/eval_jaxpr/dot_general | solution.py:28
  47.1 14.1 %fusion.39 = f32[2048,512]{1,0:T(8,128)} fusion(bf16[2048,4096]{1,0:T(8,128)(2,1)} %param.15, bf16[512,4096]{1,0:T(8,128)(2,1)S(1)} %copy-done.12), kind=kOutput, calls=%fused_computation.54 | convolution fusion | flops 8589934592 | bytes 25165824 | tf_op jit(solution)/shard_map/dot_general | solution.py:420
  65.0 1.9 constant_dynamic-slice_fusion.1.refs_3_
  66.9 1.9 constant_dynamic-slice_fusion.refs_3_
  69.7 109.8 %exchange0.1 = (bf16[2048,4096]{1,0:T(8,128)(2,1)}, f32[64,4096]{1,0:T(8,128)}, f32[64,128]{1,0:T(8,128)}) custom-call(bf16[2048,128]{1,0:T(8,128)(2,1)} %fusion.15.refs_0_, bf16[128,4096]{1,0:T(8,128)(2,1)} %bitcast.59, bf16[128,4096]{1,0:T(8,128)(2,1)} %copy-done.15, bf16[64,4096]{1,0:T(8,128)(2,1)} %constant_dynamic-slice_fusion.1.refs_3_, ...), custom_call_target="tpu_custom_call" | custom-call | flops 25769803776 | bytes 33554432 | tf_op jit(solution)/shard_map/exchange0/pallas_call | solution.py:354
  179.5 17.6 %fusion.10 = (bf16[2048,512]{1,0:T(8,128)(2,1)}, f32[2048,512]{1,0:T(8,128)S(1)}) fusion(f32[2048,512]{1,0:T(8,128)} %fusion.39, bf16[2048,4096]{1,0:T(8,128)(2,1)} %get-tuple-element.31, bf16[4096,512]{1,0:T(8,128)(2,1)} %refs_1_.2), kind=kOutput, calls=%fused_computation.22 | convolution fusion | flops 8610906112 | bytes 31457280 | tf_op jit(solution)/shard_map/dot_general | solution.py:416
  197.1 15.2 %convolution_convert_fusion = bf16[512,4096]{1,0:T(8,128)(2,1)} fusion(bf16[2048,4096]{1,0:T(8,128)(2,1)} %param.15, f32[2048,512]{1,0:T(8,128)S(1)} %get-tuple-element.39), kind=kOutput, calls=%fused_computation.11 | convolution fusion | flops 8601468928 | bytes 25165824 | tf_op jit(solution)/shard_map/dot_general | solution.py:419
  212.4 13.5 %convolution_convert_fusion.1 = bf16[4096,512]{1,0:T(8,128)(2,1)} fusion(bf16[2048,4096]{1,0:T(8,128)(2,1)S(1)} %bitcast.61, bf16[2048,512]{1,0:T(8,128)(2,1)} %get-tuple-element.38.refs_0_), kind=kOutput, calls=%fused_computation.12 | convolution fusion | flops 8592031744 | bytes 23068672 | tf_op jit(solution)/shard_map/dot_general | solution.py:422
  226.0 112.5 %exchange1.1 = (bf16[2048,4096]{1,0:T(8,128)(2,1)}, f32[64,4096]{1,0:T(8,128)}) custom-call(bf16[2048,512]{1,0:T(8,128)(2,1)} %get-tuple-element.38.refs_0_, bf16[4096,512]{1,0:T(8,128)(2,1)} %refs_1_.2, bf16[4096,512]{1,0:T(8,128)(2,1)} %collective-permute-done.1.refs_2_, bf16[64,4096]{1,0:T(8,128)(2,1)} %constant_dynamic-slice_fusion.refs_3_, ...), custom_call_target="tpu_custom_call" | custom-call | flops 103079215104 | bytes 33554432 | tf_op jit(solution)/shard_map/exchange1/pallas_call | solution.py:354
  338.5 8.3 %convolution_convert_fusion.7 = bf16[2048,128]{1,0:T(8,128)(2,1)S(1)} fusion(bf16[2048,4096]{1,0:T(8,128)(2,1)} %get-tuple-element.34, bf16[1,128,4096]{2,1,0:T(8,128)(2,1)S(1)} %copy-done.14), kind=kOutput, calls=%fused_computation.33 | convolution fusion | flops 2147745792 | bytes 18350080 | tf_op jit(solution)/shard_map/dot_general | solution.py:425
  346.9 9.2 %fusion.21 = bf16[2048,1,128]{0,2,1:T(8,128)(2,1)S(1)} fusion(bf16[2048,128]{1,0:T(8,128)(2,1)S(1)} %convolution_convert_fusion.7, f32[2048,2048]{0,1:T(8,128)} %copy-done, f32[2048]{0:T(1024)S(1)} %copy-done.8, f32[2048]{0:T(1024)S(1)} %copy-done.6), kind=kOutput, calls=%fused_computation.34 | convolution fusion | flops 1099169792 | bytes 17842176 | tf_op jit(solution)/shard_map/while/body/eval_jaxpr/dot_general | solution.py:34
  356.7 8.8 %multiply_reduce_fusion = (f32[2048]{0:T(1024)S(1)}, f32[2048,2048]{0,1:T(8,128)}) fusion(f32[2048]{0:T(1024)S(1)} %copy-done.8, f32[2048]{0:T(1024)S(1)} %copy-done.6, f32[2048,2048]{0,1:T(8,128)S(1)} %bitcast.50, bf16[2048,128]{1,0:T(8,128)(2,1)S(1)} %convolution_convert_fusion.7, bf16[2048,3,128]{0,2,1:T(8,128)(2,1)S(1)} %bitcast.55), kind=kOutput, calls=%fused_computation.2 | convolution fusion | flops 1103099904 | bytes 34627584 | tf_op jit(solution)/shard_map/while/body/eval_jaxpr/dot_general | solution.py:35
  365.5 9.7 %multiply_convert_fusion.1 = bf16[2048,2048]{0,1:T(8,128)(2,1)S(1)} fusion(f32[2048,2048]{0,1:T(8,128)} %get-tuple-element.41, f32[2048]{0:T(1024)S(1)} %get-tuple-element.40, f32[2048]{0:T(1024)S(1)} %copy-done.8, f32[2048]{0:T(1024)S(1)} %copy-done.6, f32[2048,2048]{0,1:T(8,128)S(1)} %bitcast.50), kind=kLoop, calls=%fused_computation.1 | loop fusion | flops 37748736 | bytes 41967616 | tf_op jit(solution)/shard_map/while/body/eval_jaxpr/convert_element_type | solution.py:36
  375.2 2.9 fusion.24
  379.6 1.6 copy.16.refs_0_
  381.2 9.1 %fusion.3 = bf16[1,128,4096]{2,1,0:T(8,128)(2,1)} fusion(bf16[2048,128]{1,0:T(8,128)(2,1)S(1)} %copy-done.1, bf16[2048,4096]{1,0:T(8,128)(2,1)} %get-tuple-element.34), kind=kOutput, calls=%fused_computation.15 | convolution fusion | flops 2148007936 | bytes 18350080 | tf_op jit(solution)/shard_map/dot_general | solution.py:424
  390.3 13.7 %convolution_convert_fusion.2 = bf16[4096,384]{1,0:T(8,128)(2,1)} fusion(bf16[2048,4096]{1,0:T(8,128)(2,1)} %multiply_convert_fusion, bf16[2048,384]{0,1:T(8,128)(2,1)S(1)} %bitcast.52), kind=kOutput, calls=%fused_computation.13 | convolution fusion | flops 6444023808 | bytes 21495808 | tf_op jit(solution)/shard_map/dot_general | solution.py:429
  405.4 109.6 %exchange2.1 = bf16[2048,4096]{1,0:T(8,128)(2,1)} custom-call(bf16[2048,384]{1,0:T(8,128)(2,1)} %copy.16.refs_0_, bf16[4096,384]{1,0:T(8,128)(2,1)} %refs_1_.3, bf16[4096,384]{1,0:T(8,128)(2,1)} %collective-permute-done.2.refs_2_, bf16[64,4096]{1,0:T(8,128)(2,1)} %constant_dynamic-slice_fusion.1.refs_3_, bf16[1,4096]{1,0:T(2,128)(2,1)} %broadcast_in_dim.56.refs_4_, ...), custom_call_target="tpu_custom_call" | custom-call | flops 77309411328 | bytes 33554432 | tf_op jit(solution)/shard_map/exchange2/pallas_call | solution.py:354
  515.1 14.1 %copy.18 = bf16[2048,4096]{1,0:T(8,128)(2,1)} copy(bf16[2048,4096]{1,0:T(8,128)(2,1)} %exchange2.1) | data formatting | bytes 33554432
  (64 shorter events, 10.5 us)
Async XLA Ops:
  0.6 68.1 %collective-permute-start = (bf16[128,4096]{1,0:T(8,128)(2,1)}, bf16[128,4096]{1,0:T(8,128)(2,1)S(1)}, u32[]{:S(2)}, u32[]{:S(2)}) collective-permute-start(bf16[128,4096]{1,0:T(8,128)(2,1)} %bitcast.58), channel_id=1, source_target_pairs={{0,1},{1,0},{2,3},{3,2},{4,5},{5,4},{6,7},{7,6},{8,9},{9,8},{10,11... | collective-permute-start | bytes 3145736 | tf_op jit(solution)/shard_map/ppermute | solution.py:398
  2.8 401.3 %collective-permute-start.2 = (bf16[4096,384]{1,0:T(8,128)(2,1)}, bf16[4096,384]{1,0:T(8,128)(2,1)}, u32[]{:S(2)}, u32[]{:S(2)}) collective-permute-start(bf16[4096,384]{1,0:T(8,128)(2,1)} %refs_1_.3), channel_id=1, source_target_pairs={{0,1},{1,0},{2,3},{3,2},{4,5},{5,4},{6,7},{7,6},{8,9},{9,8},{10,11... | collective-permute-start | bytes 9437192 | tf_op jit(solution)/shard_map/ppermute | solution.py:400
  2.9 223.1 %collective-permute-start.1 = (bf16[4096,512]{1,0:T(8,128)(2,1)}, bf16[4096,512]{1,0:T(8,128)(2,1)}, u32[]{:S(2)}, u32[]{:S(2)}) collective-permute-start(bf16[4096,512]{1,0:T(8,128)(2,1)} %refs_1_.2), channel_id=1, source_target_pairs={{0,1},{1,0},{2,3},{3,2},{4,5},{5,4},{6,7},{7,6},{8,9},{9,8},{10,11... | collective-permute-start | bytes 12582920 | tf_op jit(solution)/shard_map/ppermute | solution.py:399
  4.0 17.1 %copy-start.13 = (bf16[4096,384]{1,0:T(8,128)(2,1)S(1)}, bf16[4096,384]{1,0:T(8,128)(2,1)}, u32[]{:S(2)}) copy-start(bf16[4096,384]{1,0:T(8,128)(2,1)} %refs_1_.3) | copy-start | bytes 9437188
  31.8 7.1 %copy-start.2 = (bf16[2048,384]{0,1:T(8,128)(2,1)}, bf16[2048,384]{0,1:T(8,128)(2,1)S(1)}, u32[]{:S(2)}) copy-start(bf16[2048,384]{0,1:T(8,128)(2,1)S(1)} %convolution_convert_fusion.4) | copy-start | bytes 4718596
  34.2 5.7 %copy-start = (f32[2048,2048]{0,1:T(8,128)}, f32[2048,2048]{0,1:T(8,128)S(1)}, u32[]{:S(2)}) copy-start(f32[2048,2048]{0,1:T(8,128)S(1)} %get-tuple-element.37) | copy-start | bytes 50331652
  39.9 7.1 %copy-start.7 = (f32[2048]{0:T(1024)}, f32[2048]{0:T(1024)S(1)}, u32[]{:S(2)}) copy-start(f32[2048]{0:T(1024)S(1)} %fusion.1) | copy-start | bytes 24580
  39.9 7.1 %copy-start.12 = (bf16[512,4096]{1,0:T(8,128)(2,1)S(1)}, bf16[512,4096]{1,0:T(8,128)(2,1)}, u32[]{:S(2)}) copy-start(bf16[512,4096]{1,0:T(8,128)(2,1)} %param.19) | copy-start | bytes 12582916
  47.1 16.7 %copy-start.4 = (bf16[4096]{0:T(1024)(128)(2,1)S(1)}, bf16[4096]{0:T(1024)(128)(2,1)}, u32[]{:S(2)}) copy-start(bf16[4096]{0:T(1024)(128)(2,1)} %param.13) | copy-start | bytes 24580
  47.1 17.3 %copy-start.9 = (bf16[4096]{0:T(1024)(128)(2,1)S(1)}, bf16[4096]{0:T(1024)(128)(2,1)}, u32[]{:S(2)}) copy-start(bf16[4096]{0:T(1024)(128)(2,1)} %param.14) | copy-start | bytes 24580
  179.5 32.9 %slice-start.4 = ((s8[16777216]{0:T(1024)(128)(4,1)}), s8[4194304]{0:T(1024)(128)(4,1)S(1)}, s32[]{:S(2)}) async-start(s8[16777216]{0:T(1024)(128)(4,1)} %bitcast.60), calls=%async_computation.4 | async-start | bytes 8388608
  179.5 32.9 %slice-start.5 = ((s8[16777216]{0:T(1024)(128)(4,1)}), s8[4194304]{0:T(1024)(128)(4,1)S(1)}, s32[]{:S(2)}) async-start(s8[16777216]{0:T(1024)(128)(4,1)} %bitcast.60), calls=%async_computation.5 | async-start | bytes 8388608
  179.5 32.9 %slice-start.6 = ((s8[16777216]{0:T(1024)(128)(4,1)}), s8[4194304]{0:T(1024)(128)(4,1)S(1)}, s32[]{:S(2)}) async-start(s8[16777216]{0:T(1024)(128)(4,1)} %bitcast.60), calls=%async_computation.6 | async-start | bytes 8388608
  197.1 15.3 %slice-start.7 = ((s8[16777216]{0:T(1024)(128)(4,1)}), s8[4194304]{0:T(1024)(128)(4,1)S(1)}, s32[]{:S(2)}) async-start(s8[16777216]{0:T(1024)(128)(4,1)} %bitcast.60), calls=%async_computation.7 | async-start | bytes 8388608
  225.9 112.5 %copy-start.14 = (bf16[1,128,4096]{2,1,0:T(8,128)(2,1)S(1)}, bf16[1,128,4096]{2,1,0:T(8,128)(2,1)}, u32[]{:S(2)}) copy-start(bf16[1,128,4096]{2,1,0:T(8,128)(2,1)} %param.17) | copy-start | bytes 3145732
  338.4 8.4 %copy-start.6 = (f32[2048]{0:T(1024)S(1)}, f32[2048]{0:T(1024)}, u32[]{:S(2)}) copy-start(f32[2048]{0:T(1024)} %copy-done.5) | copy-start | bytes 24580
  338.4 8.4 %copy-start.8 = (f32[2048]{0:T(1024)S(1)}, f32[2048]{0:T(1024)}, u32[]{:S(2)}) copy-start(f32[2048]{0:T(1024)} %copy-done.7) | copy-start | bytes 24580
  338.4 17.7 %slice-start = ((s8[16777216]{0:T(1024)(128)(4,1)}), s8[4194304]{0:T(1024)(128)(4,1)S(1)}, s32[]{:S(2)}) async-start(s8[16777216]{0:T(1024)(128)(4,1)} %bitcast.49), calls=%async_computation | async-start | bytes 8388608
  346.8 9.3 %slice-start.1 = ((s8[16777216]{0:T(1024)(128)(4,1)}), s8[4194304]{0:T(1024)(128)(4,1)S(1)}, s32[]{:S(2)}) async-start(s8[16777216]{0:T(1024)(128)(4,1)} %bitcast.49), calls=%async_computation.1 | async-start | bytes 8388608
  346.8 9.3 %slice-start.2 = ((s8[16777216]{0:T(1024)(128)(4,1)}), s8[4194304]{0:T(1024)(128)(4,1)S(1)}, s32[]{:S(2)}) async-start(s8[16777216]{0:T(1024)(128)(4,1)} %bitcast.49), calls=%async_computation.2 | async-start | bytes 8388608
  346.8 9.4 %slice-start.3 = ((s8[16777216]{0:T(1024)(128)(4,1)}), s8[4194304]{0:T(1024)(128)(4,1)S(1)}, s32[]{:S(2)}) async-start(s8[16777216]{0:T(1024)(128)(4,1)} %bitcast.49), calls=%async_computation.3 | async-start | bytes 8388608
  346.9 9.8 %copy-start.3 = (bf16[2048,384]{0,1:T(8,128)(2,1)S(1)}, bf16[2048,384]{0,1:T(8,128)(2,1)}, u32[]{:S(2)}) copy-start(bf16[2048,384]{0,1:T(8,128)(2,1)} %copy-done.2) | copy-start | bytes 4718596
  390.3 13.7 %copy-start.11 = (f32[64]{0:T(128)S(1)}, f32[64]{0:T(128)}, u32[]{:S(2)}) copy-start(f32[64]{0:T(128)} %dynamic_slice.23) | copy-start | bytes 772
  390.3 14.4 %copy-start.10 = (f32[64]{0:T(128)S(1)}, f32[64]{0:T(128)}, u32[]{:S(2)}) copy-start(f32[64]{0:T(128)} %dynamic_slice.22) | copy-start | bytes 772
  (3 other events, 9.8 us)
